TPU v7x, 512 devices: a whole 4x4x16 slice. The times are simulated.
512 devices in a mesh: row: 16 (over x_hi, y, core), col: 32 (over x_lo, z).
Axes of the slice: x: 4 (x_hi: 2, x_lo: 2; x = x_hi * 2 + x_lo), y: 4, z: 16, core: 2. Of those that a mesh axis runs over, the one named last changes fastest.
Arguments:
- velocity_modes: bfloat16 [3, 176, 352, 704], P(None, 'row', 'col'), may hold values from -0.00090789795 to 0.00090789795
- wavenumbers: float32 [8], replicated, may hold values from 0.5 to 3
- polar: float32 [32], replicated, may hold values from -3.140625 to 3.140625
- azimuth: float32 [32], replicated, may hold values from -3.140625 to 3.140625
Outputs:
- velocity: bfloat16 [3, 512, 512, 512], P(None, 'row', 'col')
- far_field: float32 [32, 2, 8], P('col')
All inputs are finite; a program needn't handle non-finite values.
Results may differ from a plain program's by a relative error of at most 0.0075.
Values may be sent and summed in bfloat16 or wider, within the bound.
A program may use at most 64 MiB of HBM per device.

v0:
```python
import functools
import math

import jax
import jax.numpy as jnp
import numpy as np
from jax import lax
from jax.experimental import pallas as pl
from jax.experimental.pallas import tpu as pltpu
from jax.sharding import PartitionSpec as P

N = 512
M = 352
KX = 176
FREQS = 8
DIRS = 32
ROWS = 16
COLS = 32
KL = 11
BF = jnp.bfloat16
F32 = jnp.float32
MESH = pl.DeviceIdType.MESH
NT = (((1,), (1,)), ((), ()))


def tables():
    cos = np.cos(2.0 * np.pi / N * np.arange(N))
    sin = np.sin(2.0 * np.pi / N * np.arange(N))
    waves = np.arange(M) - M // 2
    grid = (waves[None, :] * np.arange(N)[:, None]) % N
    base = np.stack([cos[grid], sin[grid]], 0).reshape(2, COLS, N // COLS, M)
    one = np.zeros((COLS, 2, N // COLS, 384), np.float32)
    one[..., :M] = base.transpose(1, 0, 2, 3)
    one = one.reshape(2 * N, 384)
    grid = (waves[:, None] * np.arange(N)[None, :]) % N
    base = np.stack([cos[grid], -sin[grid]], 0)
    base = base.reshape(2, COLS, KL, ROWS, 4, 8).transpose(1, 0, 2, 4, 5, 3)
    two = np.zeros((COLS, 2, 16, N), np.float32)
    two[:, :, :KL] = base.reshape(COLS, 2, KL, N)
    two = two.reshape(COLS * 32, N)
    half = np.arange(KX)
    grid = (half[:, None] * np.arange(N)[None, :]) % N
    factor = np.where(half == 0, 1.0, 2.0)[:, None]
    base = np.stack([cos[grid], -sin[grid]], 0).astype(jnp.bfloat16).astype(np.float64) * factor
    three = np.zeros((2, ROWS, 16, N), np.float32)
    three[:, :, :KL] = base.reshape(2, ROWS, KL, N)
    three = three.reshape(2 * ROWS * 16, N)
    return [t.astype(jnp.bfloat16) for t in (one, two, three)]


def iota(shape, dim):
    return lax.broadcasted_iota(jnp.int32, shape, dim)


def chosen(condition):
    return jnp.where(condition, 1.0, 0.0)


def swapped(tiles):
    lane = iota((16, 128), 1)
    tiles = list(tiles)
    for bit in range(4):
        step = 1 << bit
        low = (lane & step) == 0
        for i in range(16):
            if i & step:
                continue
            a, b = tiles[i], tiles[i + step]
            tiles[i] = jnp.where(low, a, pltpu.roll(b, step, 1))
            tiles[i + step] = jnp.where(low, pltpu.roll(a, 128 - step, 1), b)
    return tiles


def col_peer(col, i):
    across = lax.rem(i + 1, 2)
    m = i // 2
    shift = jnp.where(m == 0, 8, jnp.where(lax.rem(m, 2) == 1, 8 - (m + 1) // 2, 8 + m // 2))
    x_lo = lax.rem(col // 16 + across, 2)
    return x_lo * 16 + lax.rem(lax.rem(col, 16) + shift, 16)


def kernel(
    modes_hbm, waves_ref, polar_ref, azimuth_ref, one_hbm, two_hbm, three_hbm,
    vel_hbm, far_ref,
    modes, padded, one, two, three, picked_re, picked_im, sent, got, lhs, mid,
    rsent, rgot, lhs_x, field, vel, phase, cos_yz, sin_yz, weights, mixed,
    fsent, fgot, gsent, ggot,
    load_sem, csend, crecv, rsend, rrecv, out_sem, fsend_sem, frecv_sem, gsend_sem, grecv_sem,
):
    row = lax.axis_index("row")
    col = lax.axis_index("col")

    barrier = pltpu.get_barrier_semaphore()

    def greet_col(i, carry):
        pl.semaphore_signal(barrier, inc=1, device_id=(row, col_peer(col, i)), device_id_type=MESH)
        return carry

    def greet_row(i, carry):
        pl.semaphore_signal(
            barrier, inc=1, device_id=(lax.rem(row + i, ROWS), col), device_id_type=MESH
        )
        return carry

    lax.fori_loop(0, COLS - 1, greet_col, 0)
    lax.fori_loop(1, ROWS, greet_row, 0)

    loads = [
        pltpu.make_async_copy(modes_hbm, modes, load_sem.at[0]),
        pltpu.make_async_copy(one_hbm, one, load_sem.at[1]),
        pltpu.make_async_copy(two_hbm, two.at[:, pl.ds(0, N)], load_sem.at[2]),
        pltpu.make_async_copy(three_hbm, three, load_sem.at[3]),
    ]
    for load in loads:
        load.start()

    padded[...] = jnp.zeros_like(padded)
    i, j = iota((128, 176), 0), iota((128, 176), 1)
    pick = chosen((i == (j // 16) * KL + lax.rem(j, 16)) & (lax.rem(j, 16) < KL)).astype(BF)
    loads[0].wait()
    for c in range(3):
        for a in range(KL):
            padded[c, a * 16 : a * 16 + KL, 0 : 2 * M] = modes[c, a]
    for c in range(3):
        rows = jnp.dot(pick, padded[c], preferred_element_type=F32)
        picked_re[c * 128 : (c + 1) * 128, :] = rows[:, :384].astype(BF)
        moved = pltpu.roll(rows, 768 - M, 1)
        picked_im[c * 128 : (c + 1) * 128, :] = moved[:, :384].astype(BF)

    loads[1].wait()

    def along_z(b, carry):
        part = one[pl.ds(pl.multiple_of(b * 256, 256), 256), :]
        pieces = []
        for g in range(8):
            pieces.append(-part[g * 32 + 16 : g * 32 + 32])
            pieces.append(part[g * 32 : g * 32 + 16])
        other = jnp.concatenate(pieces, 0)
        x = lax.dot_general(part, picked_re[...], NT, preferred_element_type=F32)
        x = x + lax.dot_general(other, picked_im[...], NT, preferred_element_type=F32)
        x = x.astype(BF)
        for c in range(3):
            sent[c, pl.ds(b * 8, 8)] = x[:, c * 128 : (c + 1) * 128].reshape(8, 32, 128)
        return carry

    lax.fori_loop(0, 4, along_z, 0)

    pl.semaphore_wait(barrier, COLS + ROWS - 2)

    def send_col(n, carry):
        c = n // (COLS - 1)
        peer = col_peer(col, lax.rem(n, COLS - 1))
        pltpu.make_async_remote_copy(
            src_ref=sent.at[c, peer], dst_ref=got.at[c, col], send_sem=csend.at[c], recv_sem=crecv.at[c],
            device_id=(row, peer), device_id_type=MESH,
        ).start()
        return carry

    lax.fori_loop(0, 3 * (COLS - 1), send_col, 0)
    for c in range(3):
        got[c, pl.ds(col, 1)] = sent[c, pl.ds(col, 1)]

    loads[2].wait()

    def fill_two(b, carry):
        base = pl.multiple_of(b * 32, 32)
        two[pl.ds(base, 16), N : 2 * N] = -two[pl.ds(base + 16, 16), 0:N]
        two[pl.ds(base + 16, 16), N : 2 * N] = two[pl.ds(base, 16), 0:N]
        return carry

    lax.fori_loop(0, COLS, fill_two, 0)

    lane = iota((8, 256), 1)
    wave = jnp.zeros((8, 256), F32)
    polar = jnp.zeros((8, 256), F32)
    azimuth = jnp.zeros((8, 256), F32)
    for m in range(FREQS):
        wave = jnp.where(lane // DIRS == m, waves_ref[m], wave)
    for d in range(DIRS):
        polar = jnp.where(lax.rem(lane, DIRS) == d, polar_ref[d], polar)
        azimuth = jnp.where(lax.rem(lane, DIRS) == d, azimuth_ref[d], azimuth)
    sin_polar = jnp.sin(polar)
    n1 = sin_polar * jnp.cos(azimuth)
    n2 = sin_polar * jnp.sin(azimuth)
    n3 = jnp.cos(polar)
    axes = (n1, n2, n3)
    third = (n1 * n1 + n2 * n2 + n3 * n3) / 3.0
    for c in range(3):
        for e in range(c + 1):
            w = axes[c] * axes[c] - third if e == c else 2.0 * axes[e] * axes[c]
            weights[c, e, :, 0:256] = w
            weights[c, e, :, 256:512] = w
    unit = 2.0 * math.pi / N
    wave_1, one_1, two_1, three_1 = wave[0:1], n1[0:1], n2[0:1], n3[0:1]

    def phases(b, carry):
        base = pl.multiple_of(b * 32, 32)
        index = iota((32, 256), 0) + base
        angle = wave_1 * (one_1 * (index.astype(F32) * unit))
        phase[pl.ds(base, 32), 0:256] = jnp.cos(angle).astype(BF)
        phase[pl.ds(base, 32), 256:512] = (-jnp.sin(angle)).astype(BF)
        y_pos = (row * 32 + index // 16).astype(F32) * unit
        z_pos = (col * 16 + lax.rem(index, 16)).astype(F32) * unit
        angle = wave_1 * (two_1 * y_pos) + wave_1 * (three_1 * z_pos)
        cos_yz[pl.ds(base, 32), :] = jnp.cos(angle)
        sin_yz[pl.ds(base, 32), :] = jnp.sin(angle)
        return carry

    lax.fori_loop(0, 16, phases, 0)
    mixed[...] = jnp.zeros_like(mixed)

    i, j = iota((176, 128), 0), iota((176, 128), 1)
    spread = chosen((j == lax.rem(i, 16) * KL + i // 16) & (lax.rem(i, 16) < KL)).astype(BF)
    turn = chosen(iota((128, 128), 0) == iota((128, 128), 1)).astype(BF)
    loads[3].wait()

    def step(c, carry):
        @pl.when(c < 3)
        def _():
            pltpu.make_async_copy(
                got.at[c, pl.ds(0, COLS - 1)], got.at[c, pl.ds(0, COLS - 1)], crecv.at[c]
            ).wait()
            def regroup(t, carry):
                lines = got[c, pl.ds(t * 4, 4)].reshape(128, 128)
                turned = lax.dot_general(spread, lines, NT, preferred_element_type=F32)
                zero = jnp.zeros((16, 128), F32)
                tiles = [turned[k * 16 : k * 16 + 16] for k in range(KL)] + [zero] * (16 - KL)
                for k, tile in enumerate(swapped(tiles)):
                    lhs[t, k * 16 : k * 16 + 16, :] = tile.astype(BF)
                return carry

            lax.fori_loop(0, 8, regroup, 0)
            wide = jnp.concatenate([lhs[t] for t in range(8)], 1)
            out = jnp.dot(wide, two[...], preferred_element_type=F32)
            for t in range(8):
                mid[t] = out[:, t * 128 : (t + 1) * 128].astype(BF)

            def regroup_row(t, carry):
                tiles = [mid[t, k * 16 : k * 16 + 16, :].astype(F32) for k in range(16)]
                for k, tile in enumerate(swapped(tiles)):
                    rsent[c, k, t] = tile.astype(BF)
                return carry

            lax.fori_loop(0, 8, regroup_row, 0)

            def send_row(k, carry):
                peer = lax.rem(row + k, ROWS)
                pltpu.make_async_remote_copy(
                    src_ref=rsent.at[c, peer], dst_ref=rgot.at[c, row],
                    send_sem=rsend.at[c], recv_sem=rrecv.at[c],
                    device_id=(peer, col), device_id_type=MESH,
                ).start()
                return carry

            lax.fori_loop(1, ROWS, send_row, 0)
            rgot[c, pl.ds(row, 1)] = rsent[c, pl.ds(row, 1)]

        @pl.when(c > 0)
        def _():
            e = c - 1
            pltpu.make_async_copy(
                rgot.at[e, pl.ds(0, ROWS - 1)], rgot.at[e, pl.ds(0, ROWS - 1)], rrecv.at[e]
            ).wait()
            for h in range(4):
                for p in range(2):
                    block = rgot[e, :, p * 4 + h].reshape(256, 128)
                    turned = lax.dot_general(turn, block, NT, preferred_element_type=F32)
                    lhs_x[h * 128 : (h + 1) * 128, p * 256 : (p + 1) * 256] = turned.astype(BF)
            field[e] = jnp.dot(lhs_x[...], three[...], preferred_element_type=F32)
            vel[e] = field[e].astype(BF)
            pltpu.make_async_copy(vel.at[e], vel_hbm.at[e], out_sem.at[e]).start()

            def component(g, carry):
                stress = (field[e] * field[g]).astype(BF)
                lines = jnp.dot(stress, phase[...], preferred_element_type=F32)
                mixed[...] += weights[e, g, 0:1, :] * lines
                return carry

            lax.fori_loop(0, e + 1, component, 0)

        return carry

    lax.fori_loop(0, 4, step, 0)

    re, im = mixed[:, 0:256], mixed[:, 256:512]
    cosine, sine = cos_yz[...], sin_yz[...]
    sum_re = jnp.sum(re * cosine + im * sine, axis=0, keepdims=True)
    sum_im = jnp.sum(im * cosine - re * sine, axis=0, keepdims=True)
    mine = lax.rem(iota((DIRS, 256), 1), DIRS) == iota((DIRS, 256), 0)
    i, j = iota((256, 128), 0) // DIRS, iota((256, 128), 1)
    dot = functools.partial(jnp.dot, preferred_element_type=F32, precision=lax.Precision.HIGHEST)
    per_dir = dot(jnp.where(mine, sum_re, 0.0), chosen(i == j))
    per_dir = per_dir + dot(jnp.where(mine, sum_im, 0.0), chosen(i + FREQS == j))
    for d in range(DIRS):
        fsent[d] = per_dir[d : d + 1]

    def send_far(k, carry):
        peer = col_peer(col, k)
        pltpu.make_async_remote_copy(
            src_ref=fsent.at[peer], dst_ref=fgot.at[col], send_sem=fsend_sem, recv_sem=frecv_sem,
            device_id=(row, peer), device_id_type=MESH,
        ).start()
        return carry

    lax.fori_loop(0, COLS - 1, send_far, 0)
    fgot[pl.ds(col, 1)] = fsent[pl.ds(col, 1)]
    pltpu.make_async_copy(
        fgot.at[pl.ds(0, COLS - 1)], fgot.at[pl.ds(0, COLS - 1)], frecv_sem
    ).wait()
    gsent[...] = jnp.sum(fgot[...], axis=0)

    def send_all(k, carry):
        peer = lax.rem(row + k, ROWS)
        pltpu.make_async_remote_copy(
            src_ref=gsent, dst_ref=ggot.at[row], send_sem=gsend_sem, recv_sem=grecv_sem,
            device_id=(peer, col), device_id_type=MESH,
        ).start()
        return carry

    lax.fori_loop(1, ROWS, send_all, 0)
    ggot[pl.ds(row, 1)] = gsent[...][None]
    pltpu.make_async_copy(
        ggot.at[pl.ds(0, ROWS - 1)], ggot.at[pl.ds(0, ROWS - 1)], grecv_sem
    ).wait()
    total = jnp.sum(ggot[...], axis=0)
    lane = iota((1, 128), 1)
    wave = jnp.zeros((1, 128), F32)
    for m in range(FREQS):
        wave = jnp.where(lax.rem(lane, FREQS) == m, waves_ref[m], wave)
    total = total * (wave * wave) / N**1.5
    far_ref[0, 0:1, :] = total[:, 0:FREQS]
    far_ref[0, 1:2, :] = total[:, FREQS : 2 * FREQS]

    for c in range(3):
        pltpu.make_async_copy(
            sent.at[c, pl.ds(0, COLS - 1)], sent.at[c, pl.ds(0, COLS - 1)], csend.at[c]
        ).wait()
        pltpu.make_async_copy(
            rsent.at[c, pl.ds(0, ROWS - 1)], rsent.at[c, pl.ds(0, ROWS - 1)], rsend.at[c]
        ).wait()
        pltpu.make_async_copy(vel.at[c], vel_hbm.at[c], out_sem.at[c]).wait()
    pltpu.make_async_copy(
        fsent.at[pl.ds(0, COLS - 1)], fsent.at[pl.ds(0, COLS - 1)], fsend_sem
    ).wait()
    pltpu.make_async_copy(
        ggot.at[pl.ds(0, ROWS - 1)], ggot.at[pl.ds(0, ROWS - 1)], gsend_sem
    ).wait()


def body(velocity_modes, wavenumbers, polar, azimuth):
    one, two, three = tables()
    any_space = pl.BlockSpec(memory_space=pl.ANY)
    scalars = pl.BlockSpec(memory_space=pltpu.SMEM)
    dma = pltpu.SemaphoreType.DMA
    velocity, far = pl.pallas_call(
        kernel,
        out_shape=(
            jax.ShapeDtypeStruct((3, N, N), BF),
            jax.ShapeDtypeStruct((1, 2, FREQS), F32),
        ),
        in_specs=[any_space, scalars, scalars, scalars, any_space, any_space, any_space],
        out_specs=(any_space, pl.BlockSpec(memory_space=pltpu.VMEM)),
        scratch_shapes=[
            pltpu.VMEM((3, KL, KL, 2 * M), BF),
            pltpu.VMEM((3, 176, 768), BF),
            pltpu.VMEM((2 * N, 384), BF),
            pltpu.VMEM((2 * N, 2 * N), BF),
            pltpu.VMEM((N, N), BF),
            pltpu.VMEM((384, 384), BF),
            pltpu.VMEM((384, 384), BF),
            pltpu.VMEM((3, COLS, 32, 128), BF),
            pltpu.VMEM((3, COLS, 32, 128), BF),
            pltpu.VMEM((8, 256, 128), BF),
            pltpu.VMEM((8, 256, 128), BF),
            pltpu.VMEM((3, ROWS, 8, 16, 128), BF),
            pltpu.VMEM((3, ROWS, 8, 16, 128), BF),
            pltpu.VMEM((N, N), BF),
            pltpu.VMEM((3, N, N), F32),
            pltpu.VMEM((3, N, N), BF),
            pltpu.VMEM((N, N), BF),
            pltpu.VMEM((N, 256), F32),
            pltpu.VMEM((N, 256), F32),
            pltpu.VMEM((3, 3, 8, N), F32),
            pltpu.VMEM((N, N), F32),
            pltpu.VMEM((COLS, 1, 128), F32),
            pltpu.VMEM((COLS, 1, 128), F32),
            pltpu.VMEM((1, 128), F32),
            pltpu.VMEM((ROWS, 1, 128), F32),
            dma((4,)),
            dma((3,)),
            dma((3,)),
            dma((3,)),
            dma((3,)),
            dma((3,)),
            dma,
            dma,
            dma,
            dma,
        ],
        compiler_params=pltpu.CompilerParams(
            collective_id=0, has_side_effects=True, vmem_limit_bytes=48 * 1024 * 1024
        ),
    )(velocity_modes, wavenumbers, polar, azimuth, jnp.asarray(one), jnp.asarray(two), jnp.asarray(three))
    return velocity.reshape(3, N // ROWS, N // COLS, N), far


def solution(mesh):
    in_specs = (P(None, "row", "col", None), P(), P(), P())
    out_specs = (P(None, "row", "col", None), P("col", None, None))
    return jax.shard_map(body, mesh=mesh, in_specs=in_specs, out_specs=out_specs, check_vma=False)
```

profile of v0, /device:TPU:1, one launch (start us, length us, event | category | flops | bytes accessed | tf_op | source)
XLA Modules:
  0.0 92.1 jit_solution(1430820126235231315)
XLA Ops:
  0.6 0.0 copy-start
  0.6 1.3 %copy.9.modes_hbm = bf16[3,11,11,704]{3,2,1,0:T(8,128)(2,1)S(1)} copy(bf16[3,11,11,704]{3,0,2,1:T(4,128)(2,1)} %param.7) | data formatting | bytes 1022208 | tf_op args[0]
  1.9 0.1 copy-done
  2.1 0.0 copy-start.1
  2.1 1.1 %copy-done.1 = bf16[1024,384]{1,0:T(8,128)(2,1)S(1)} copy-done((bf16[1024,384]{1,0:T(8,128)(2,1)S(1)}, bf16[1024,384]{1,0:T(8,128)(2,1)}, u32[]{:S(2)}) %copy-start.1) | copy-done | bytes 786456
  3.2 0.0 copy-start.2
  3.2 1.0 %copy-done.2 = bf16[512,512]{1,0:T(8,128)(2,1)S(1)} copy-done((bf16[512,512]{1,0:T(8,128)(2,1)S(1)}, bf16[512,512]{1,0:T(8,128)(2,1)}, u32[]{:S(2)}) %copy-start.2) | copy-done | bytes 524312
  4.3 0.0 copy-start.3
  4.3 0.7 copy-done.3
  4.9 0.0 copy-start.4
  4.9 0.7 copy-done.4
  5.6 0.0 copy-start.5
  5.6 0.7 copy-done.5
  6.2 84.1 %shard_map.86 = (bf16[3,512,512]{2,1,0:T(8,128)(2,1)S(1)}, f32[1,2,8]{2,1,0:T(2,128)S(1)}) custom-call(bf16[3,11,11,704]{3,2,1,0:T(8,128)(2,1)S(1)} %copy.9.modes_hbm, f32[8]{0:T(128)S(1)} %copy-done.3, f32[32]{0:T(128)S(1)} %copy-done.4, f32[32]{0:T(128)S(1)} %copy-done.5, bf16[1024,384]{1,0:T(8,128)(2,1)S(1)} %copy-done.1, bf16[1024,512]{1,0:T(8,128)(2,1)S(1)} %copy-done, ...), custom_call_target="tpu_custom_call" | custom-call | tf_op jit(solution)/shard_map/pallas_call | solution.py:355
  90.3 1.1 %copy.12 = bf16[3,32,16,512]{3,2,1,0:T(8,128)(2,1)} copy(bf16[3,32,16,512]{3,2,1,0:T(8,128)(2,1)S(1)} %bitcast.1) | data formatting | bytes 3145728
  91.5 0.6 copy.13
Async XLA Ops:
  0.6 1.5 %copy-start = (bf16[1024,512]{1,0:T(8,128)(2,1)S(1)}, bf16[1024,512]{1,0:T(8,128)(2,1)}, u32[]{:S(2)}) copy-start(bf16[1024,512]{1,0:T(8,128)(2,1)} %constant.7.clone.two_hbm) | copy-start | bytes 3145732
  2.1 1.1 %copy-start.1 = (bf16[1024,384]{1,0:T(8,128)(2,1)S(1)}, bf16[1024,384]{1,0:T(8,128)(2,1)}, u32[]{:S(2)}) copy-start(bf16[1024,384]{1,0:T(8,128)(2,1)} %constant.6.clone.one_hbm) | copy-start | bytes 2359300
  3.2 1.0 %copy-start.2 = (bf16[512,512]{1,0:T(8,128)(2,1)S(1)}, bf16[512,512]{1,0:T(8,128)(2,1)}, u32[]{:S(2)}) copy-start(bf16[512,512]{1,0:T(8,128)(2,1)} %constant.8.clone.three_hbm) | copy-start | bytes 1572868
  4.3 0.7 copy-start.3
  4.9 0.7 copy-start.4
  5.6 0.7 copy-start.5
where the time goes:
time: 92.3 us; the launch traced here: 92.1 us
  Pallas kernels  84.1 us (91%)
  local copies, waits for them, and re-layouts  7.28 us (8%)
    pallas_call x1, Pallas kernels, body(): pl.pallas_call(kernel, out_shape=(jax.ShapeDtypeStruct((3, N, N), BF), ja...  84.1 us
    unnamed x15, local copies, waits for them, and re-layouts  7.28 us

commit v1 on v0

v1 whole, which is shorter than its diff:
```python
import functools
import math

import jax
import jax.numpy as jnp
import numpy as np
from jax import lax
from jax.experimental import pallas as pl
from jax.experimental.pallas import tpu as pltpu
from jax.sharding import PartitionSpec as P

N = 512
M = 352
KX = 176
FREQS = 8
DIRS = 32
ROWS = 16
COLS = 32
KL = 11
BF = jnp.bfloat16
F32 = jnp.float32
MESH = pl.DeviceIdType.MESH
NT = (((1,), (1,)), ((), ()))


def tables():
    cos = np.cos(2.0 * np.pi / N * np.arange(N))
    sin = np.sin(2.0 * np.pi / N * np.arange(N))
    waves = np.arange(M) - M // 2
    grid = (waves[None, :] * np.arange(N)[:, None]) % N
    base = np.stack([cos[grid], sin[grid]], 0).reshape(2, COLS, 2, 8, M)
    one = np.zeros((2, 2, COLS, 8, 384), np.float32)
    one[..., :M] = base.transpose(0, 2, 1, 3, 4)
    one = one.reshape(2, N, 384)
    grid = (waves[:, None] * np.arange(N)[None, :]) % N
    base = np.zeros((2, COLS, 16, N))
    base[:, :, :KL] = np.stack([cos[grid], -sin[grid]], 0).reshape(2, COLS, KL, N)
    two = base.reshape(2, COLS, 2, 8, 2, 8, 2, 16).transpose(2, 1, 0, 3, 4, 6, 7, 5).reshape(2 * N, N)
    half = np.arange(KX)
    grid = (half[:, None] * np.arange(N)[None, :]) % N
    factor = np.where(half == 0, 1.0, 2.0)[:, None]
    base = np.stack([cos[grid], -sin[grid]], 0).astype(jnp.bfloat16).astype(np.float64) * factor
    three = np.zeros((2, ROWS, 16, N), np.float32)
    three[:, :, :KL] = base.reshape(2, ROWS, KL, N)
    three = three.reshape(2 * ROWS * 16, N)
    return [t.astype(jnp.bfloat16) for t in (one, two, three)]


def iota(shape, dim):
    return lax.broadcasted_iota(jnp.int32, shape, dim)


def chosen(condition):
    return jnp.where(condition, 1.0, 0.0)


def swapped(tiles):
    lane = iota((16, 128), 1)
    tiles = list(tiles)
    for bit in range(3):
        step = 1 << bit
        low = lax.rem(lane // step, 2) == 0
        for i in range(8):
            if (i // step) % 2:
                continue
            a, b = tiles[i], tiles[i + step]
            tiles[i] = jnp.where(low, a, pltpu.roll(b, step, 1))
            tiles[i + step] = jnp.where(low, pltpu.roll(a, 128 - step, 1), b)
    return tiles


SHIFTS = (8, 7, 9, 6, 10, 5, 11, 4, 12, 3, 13, 2, 14, 1, 15, 0)


def col_peers(col):
    base = lax.div(col, 16) * 16
    z = col - base
    peers = []
    for shift in SHIFTS:
        there = lax.rem(z + shift, 16)
        peers.append((16 - base) + there)
        if shift:
            peers.append(base + there)
    return peers


def kernel(
    modes_hbm, waves_hbm, polar_hbm, azimuth_hbm, one_hbm, two_hbm, three_hbm,
    vel_hbm, far_ref,
    waves_ref, polar_ref, azimuth_ref,
    modes, padded, one, two, three, picked_re, picked_im, sent, got, lhs, mid,
    rsent, rgot, lhs_x, field, vel, phase, cos_yz, sin_yz, weights, mixed, spectrum,
    fsent, fgot, gsent, ggot,
    load_sem, csend, crecv, rsend, rrecv, out_sem, fsend_sem, frecv_sem, gsend_sem, grecv_sem,
):
    row = lax.axis_index("row")
    col = lax.axis_index("col")
    peers = col_peers(col)
    row_peers = [lax.rem(row + k, ROWS) for k in range(1, ROWS)]

    barrier = pltpu.get_barrier_semaphore()
    for peer in peers:
        pl.semaphore_signal(barrier, inc=1, device_id=(row, peer), device_id_type=MESH)
    for peer in row_peers:
        pl.semaphore_signal(barrier, inc=1, device_id=(peer, col), device_id_type=MESH)

    loads = [
        pltpu.make_async_copy(modes_hbm, modes, load_sem.at[0]),
        pltpu.make_async_copy(one_hbm, one, load_sem.at[1]),
        pltpu.make_async_copy(two_hbm, two.at[:, pl.ds(0, N)], load_sem.at[2]),
        pltpu.make_async_copy(three_hbm, three, load_sem.at[3]),
        pltpu.make_async_copy(waves_hbm, waves_ref, load_sem.at[4]),
        pltpu.make_async_copy(polar_hbm, polar_ref, load_sem.at[5]),
        pltpu.make_async_copy(azimuth_hbm, azimuth_ref, load_sem.at[6]),
    ]
    for load in loads:
        load.start()

    padded[...] = jnp.zeros_like(padded)
    i, j = iota((384, 488), 0), iota((384, 488), 1)
    pick = chosen((j // 4 == lax.rem(i, 128)) & (lax.rem(j, 4) == i // 128) & (j < 4 * KL * KL)).astype(BF)
    loads[0].wait()
    for a in range(KL):
        for b in range(KL):
            k = (a * KL + b) * 4
            padded[k : k + 3, 0 : 2 * M] = modes[a, b].astype(F32)
    rows = jnp.dot(pick, padded[...].astype(BF), preferred_element_type=F32)
    picked_re[...] = rows[:, :384].astype(BF)
    moved = pltpu.roll(rows, 768 - M, 1)
    picked_im[...] = moved[:, :384].astype(BF)

    loads[1].wait()
    nt = functools.partial(lax.dot_general, dimension_numbers=NT, preferred_element_type=F32)

    def along_z(h, carry):
        cosine = one[0, pl.ds(h * 256, 256), :]
        sine = one[1, pl.ds(h * 256, 256), :]
        x_re = nt(cosine, picked_re[...]) - nt(sine, picked_im[...])
        x_im = nt(sine, picked_re[...]) + nt(cosine, picked_im[...])
        x = jnp.concatenate([x_re.reshape(COLS, 8, 384), x_im.reshape(COLS, 8, 384)], 1).astype(BF)
        for c in range(3):
            sent[h * 3 + c] = x[:, :, c * 128 : (c + 1) * 128]

        @pl.when(h == 0)
        def _():
            pl.semaphore_wait(barrier, COLS + ROWS - 2)

        def send_col(c, carry):
            n = h * 3 + c
            for peer in peers:
                pltpu.make_async_remote_copy(
                    src_ref=sent.at[n, peer], dst_ref=got.at[n, col],
                    send_sem=csend.at[n], recv_sem=crecv.at[n],
                    device_id=(row, peer), device_id_type=MESH,
                ).start()
            got[n, pl.ds(col, 1)] = sent[n, pl.ds(col, 1)]
            return carry

        lax.fori_loop(0, 3, send_col, 0)
        return carry

    lax.fori_loop(0, 2, along_z, 0)

    loads[2].wait()

    def fill_two(b, carry):
        base = pl.multiple_of(b * 64, 64)
        half = two[pl.ds(base, 64), 0:N].astype(F32).reshape(4, 2, 8, N)
        other = jnp.concatenate([-half[:, 1:2], half[:, 0:1]], 1)
        two[pl.ds(base, 64), N : 2 * N] = other.reshape(64, N).astype(BF)
        return carry

    lax.fori_loop(0, 16, fill_two, 0)
    for load in loads[4:]:
        load.wait()

    lane = iota((8, 256), 1)
    wave = jnp.zeros((8, 256), F32)
    polar = jnp.zeros((8, 256), F32)
    azimuth = jnp.zeros((8, 256), F32)
    for m in range(FREQS):
        wave = jnp.where(lane // DIRS == m, waves_ref[m], wave)
    for d in range(DIRS):
        polar = jnp.where(lax.rem(lane, DIRS) == d, polar_ref[d], polar)
        azimuth = jnp.where(lax.rem(lane, DIRS) == d, azimuth_ref[d], azimuth)
    sin_polar = jnp.sin(polar)
    n1 = sin_polar * jnp.cos(azimuth)
    n2 = sin_polar * jnp.sin(azimuth)
    n3 = jnp.cos(polar)
    axes = (n1, n2, n3)
    third = (n1 * n1 + n2 * n2 + n3 * n3) / 3.0
    for c in range(3):
        for e in range(c + 1):
            w = axes[c] * axes[c] - third if e == c else 2.0 * axes[e] * axes[c]
            weights[c, e, :, 0:256] = w
            weights[c, e, :, 256:512] = w
    unit = 2.0 * math.pi / N
    wave_1, one_1, two_1, three_1 = wave[0:1], n1[0:1], n2[0:1], n3[0:1]

    def phases(b, carry):
        base = pl.multiple_of(b * 32, 32)
        index = iota((32, 256), 0) + base
        angle = wave_1 * (one_1 * (index.astype(F32) * unit))
        phase[pl.ds(base, 32), 0:256] = jnp.cos(angle).astype(BF)
        phase[pl.ds(base, 32), 256:512] = (-jnp.sin(angle)).astype(BF)
        part = lax.rem(index, 256)
        y_pos = (row * 32 + part // 8).astype(F32) * unit
        z_pos = (col * 16 + (index // 256) * 8 + lax.rem(part, 8)).astype(F32) * unit
        angle = wave_1 * (two_1 * y_pos) + wave_1 * (three_1 * z_pos)
        cos_yz[pl.ds(base, 32), :] = jnp.cos(angle)
        sin_yz[pl.ds(base, 32), :] = jnp.sin(angle)
        return carry

    lax.fori_loop(0, 16, phases, 0)
    mixed[...] = jnp.zeros_like(mixed)
    spectrum[...] = jnp.zeros_like(spectrum)

    i, j = iota((176, 128), 0), iota((176, 128), 1)
    spread = chosen((j == lax.rem(i, 16) * KL + i // 16) & (lax.rem(i, 16) < KL)).astype(BF)
    turn = chosen(iota((128, 128), 0) == iota((128, 128), 1)).astype(BF)
    loads[3].wait()

    def step(n, carry):
        @pl.when(n < 6)
        def _():
            pltpu.make_async_copy(
                got.at[n, pl.ds(0, COLS - 1)], got.at[n, pl.ds(0, COLS - 1)], crecv.at[n]
            ).wait()

            def regroup(pair, carry):
                for k in range(2):
                    t = pair * 2 + k
                    lines = got[n, pl.ds(t * 8, 8)].reshape(128, 128)
                    turned = nt(spread, lines).astype(BF)
                    zero = jnp.zeros((16, 128), BF)
                    tiles = [turned[m * 16 : m * 16 + 16] for m in range(KL)] + [zero] * (16 - KL)
                    for m, tile in enumerate(swapped(tiles[:8])):
                        lhs[t, m * 16 : m * 16 + 16, :] = tile
                    for m, tile in enumerate(swapped(tiles[8:])):
                        lhs[t + 4, m * 16 : m * 16 + 16, :] = tile
                return carry

            lax.fori_loop(0, 2, regroup, 0)
            wide = jnp.concatenate([lhs[t] for t in range(8)], 1)
            out = jnp.dot(wide, two[...], preferred_element_type=F32)
            for t in range(8):
                mid[t] = out[:, t * 128 : (t + 1) * 128].astype(BF)

            def regroup_row(part, carry):
                for upper in range(2):
                    for y_upper in range(2):
                        t = part * 4 + upper * 2 + y_upper
                        tiles = [mid[t, k * 16 : k * 16 + 16, :] for k in range(8)]
                        for k, tile in enumerate(swapped(tiles)):
                            rsent[n, upper * 8 + k, part * 2 + y_upper] = tile
                return carry

            lax.fori_loop(0, 2, regroup_row, 0)
            for peer in row_peers:
                pltpu.make_async_remote_copy(
                    src_ref=rsent.at[n, peer], dst_ref=rgot.at[n, row],
                    send_sem=rsend.at[n], recv_sem=rrecv.at[n],
                    device_id=(peer, col), device_id_type=MESH,
                ).start()
            rgot[n, pl.ds(row, 1)] = rsent[n, pl.ds(row, 1)]

        @pl.when(n > 0)
        def _():
            e = n - 1
            h = lax.div(e, 3)
            c = e - 3 * h
            pltpu.make_async_copy(
                rgot.at[e, pl.ds(0, ROWS - 1)], rgot.at[e, pl.ds(0, ROWS - 1)], rrecv.at[e]
            ).wait()
            for y_upper in range(2):
                for p in range(2):
                    block = rgot[e, :, p * 2 + y_upper].reshape(256, 128)
                    lhs_x[y_upper * 128 : (y_upper + 1) * 128, p * 256 : (p + 1) * 256] = nt(turn, block).astype(BF)
            field[c] = jnp.dot(lhs_x[...], three[...], preferred_element_type=F32)
            vel[e] = field[c].reshape(32, 8, N).astype(BF)
            pltpu.make_async_copy(vel.at[e], vel_hbm.at[c, :, pl.ds(h * 8, 8), :], out_sem.at[e]).start()

            def component(g, carry):
                stress = (field[c] * field[g]).astype(BF)
                lines = jnp.dot(stress, phase[...], preferred_element_type=F32)
                mixed[...] += weights[c, g, 0:1, :] * lines
                return carry

            lax.fori_loop(0, c + 1, component, 0)

            @pl.when(c == 2)
            def _():
                re, im = mixed[:, 0:256], mixed[:, 256:512]
                cosine, sine = cos_yz[pl.ds(h * 256, 256), :], sin_yz[pl.ds(h * 256, 256), :]
                spectrum[0:1, :] += jnp.sum(re * cosine + im * sine, axis=0, keepdims=True)
                spectrum[1:2, :] += jnp.sum(im * cosine - re * sine, axis=0, keepdims=True)
                mixed[...] = jnp.zeros_like(mixed)

        return carry

    lax.fori_loop(0, 7, step, 0)

    sum_re, sum_im = spectrum[0:1, :], spectrum[1:2, :]
    mine = lax.rem(iota((DIRS, 256), 1), DIRS) == iota((DIRS, 256), 0)
    i, j = iota((256, 128), 0) // DIRS, iota((256, 128), 1)
    dot = functools.partial(jnp.dot, preferred_element_type=F32, precision=lax.Precision.HIGHEST)
    per_dir = dot(jnp.where(mine, sum_re, 0.0), chosen(i == j))
    per_dir = per_dir + dot(jnp.where(mine, sum_im, 0.0), chosen(i + FREQS == j))
    for d in range(DIRS):
        fsent[d] = per_dir[d : d + 1]

    for peer in peers:
        pltpu.make_async_remote_copy(
            src_ref=fsent.at[peer], dst_ref=fgot.at[col], send_sem=fsend_sem, recv_sem=frecv_sem,
            device_id=(row, peer), device_id_type=MESH,
        ).start()
    fgot[pl.ds(col, 1)] = fsent[pl.ds(col, 1)]
    pltpu.make_async_copy(
        fgot.at[pl.ds(0, COLS - 1)], fgot.at[pl.ds(0, COLS - 1)], frecv_sem
    ).wait()
    gsent[...] = jnp.sum(fgot[...], axis=0)

    for peer in row_peers:
        pltpu.make_async_remote_copy(
            src_ref=gsent, dst_ref=ggot.at[row], send_sem=gsend_sem, recv_sem=grecv_sem,
            device_id=(peer, col), device_id_type=MESH,
        ).start()
    ggot[pl.ds(row, 1)] = gsent[...][None]
    pltpu.make_async_copy(
        ggot.at[pl.ds(0, ROWS - 1)], ggot.at[pl.ds(0, ROWS - 1)], grecv_sem
    ).wait()
    total = jnp.sum(ggot[...], axis=0)
    lane = iota((1, 128), 1)
    wave = jnp.zeros((1, 128), F32)
    for m in range(FREQS):
        wave = jnp.where(lax.rem(lane, FREQS) == m, waves_ref[m], wave)
    total = total * (wave * wave) / N**1.5
    far_ref[0, 0:1, :] = total[:, 0:FREQS]
    far_ref[0, 1:2, :] = total[:, FREQS : 2 * FREQS]

    for c in range(6):
        pltpu.make_async_copy(
            sent.at[c, pl.ds(0, COLS - 1)], sent.at[c, pl.ds(0, COLS - 1)], csend.at[c]
        ).wait()
        pltpu.make_async_copy(
            rsent.at[c, pl.ds(0, ROWS - 1)], rsent.at[c, pl.ds(0, ROWS - 1)], rsend.at[c]
        ).wait()
        pltpu.make_async_copy(vel.at[c], vel_hbm.at[c % 3, :, pl.ds(c // 3 * 8, 8), :], out_sem.at[c]).wait()
    pltpu.make_async_copy(
        fsent.at[pl.ds(0, COLS - 1)], fsent.at[pl.ds(0, COLS - 1)], fsend_sem
    ).wait()
    pltpu.make_async_copy(
        ggot.at[pl.ds(0, ROWS - 1)], ggot.at[pl.ds(0, ROWS - 1)], gsend_sem
    ).wait()


def body(velocity_modes, wavenumbers, polar, azimuth):
    one, two, three = tables()
    hbm = pl.BlockSpec(memory_space=pltpu.HBM)
    dma = pltpu.SemaphoreType.DMA
    return pl.pallas_call(
        kernel,
        out_shape=(
            jax.ShapeDtypeStruct((3, N // ROWS, N // COLS, N), BF),
            jax.ShapeDtypeStruct((1, 2, FREQS), F32),
        ),
        in_specs=[hbm] * 7,
        out_specs=(pl.BlockSpec(memory_space=pl.ANY), pl.BlockSpec(memory_space=pltpu.VMEM)),
        scratch_shapes=[
            pltpu.SMEM((FREQS,), F32),
            pltpu.SMEM((DIRS,), F32),
            pltpu.SMEM((DIRS,), F32),
            pltpu.VMEM((KL, KL, 3, 2 * M), BF),
            pltpu.VMEM((488, 768), F32),
            pltpu.VMEM((2, N, 384), BF),
            pltpu.VMEM((2 * N, 2 * N), BF),
            pltpu.VMEM((N, N), BF),
            pltpu.VMEM((384, 384), BF),
            pltpu.VMEM((384, 384), BF),
            pltpu.VMEM((6, COLS, 16, 128), BF),
            pltpu.VMEM((6, COLS, 16, 128), BF),
            pltpu.VMEM((8, 128, 128), BF),
            pltpu.VMEM((8, 128, 128), BF),
            pltpu.VMEM((6, ROWS, 4, 16, 128), BF),
            pltpu.VMEM((6, ROWS, 4, 16, 128), BF),
            pltpu.VMEM((256, N), BF),
            pltpu.VMEM((3, 256, N), F32),
            pltpu.VMEM((6, 32, 8, N), BF),
            pltpu.VMEM((N, N), BF),
            pltpu.VMEM((N, 256), F32),
            pltpu.VMEM((N, 256), F32),
            pltpu.VMEM((3, 3, 8, N), F32),
            pltpu.VMEM((256, N), F32),
            pltpu.VMEM((8, 256), F32),
            pltpu.VMEM((COLS, 1, 128), F32),
            pltpu.VMEM((COLS, 1, 128), F32),
            pltpu.VMEM((1, 128), F32),
            pltpu.VMEM((ROWS, 1, 128), F32),
            dma((7,)),
            dma((6,)),
            dma((6,)),
            dma((6,)),
            dma((6,)),
            dma((6,)),
            dma,
            dma,
            dma,
            dma,
        ],
        compiler_params=pltpu.CompilerParams(
            collective_id=0, has_side_effects=True, vmem_limit_bytes=67043328
        ),
    )(jnp.transpose(velocity_modes, (1, 2, 0, 3)), wavenumbers, polar, azimuth, jnp.asarray(one), jnp.asarray(two), jnp.asarray(three))


def solution(mesh):
    in_specs = (P(None, "row", "col", None), P(), P(), P())
    out_specs = (P(None, "row", "col", None), P("col", None, None))
    return jax.shard_map(body, mesh=mesh, in_specs=in_specs, out_specs=out_specs, check_vma=False)
```

time: 92.3 us -> 81.3 us (0.88)
  Pallas kernels: 84.1 us -> 77.3 us
  local copies, waits for them, and re-layouts: 7.28 us -> 3.24 us
    pallas_call x1, Pallas kernels: 84.1 us -> 77.3 us  [body(): pl.pallas_call(kernel, out_shape=(jax.ShapeDtypeStruct((3, N // ROWS, N /...]
    unnamed x15 -> x4, local copies, waits for them, and re-layouts: 7.28 us -> 3.24 us
where the time goes in v1:
time: 81.3 us; the launch traced here: 81.1 us
  Pallas kernels  77.3 us (95%)
  local copies, waits for them, and re-layouts  3.24 us (4%)
    pallas_call x1, Pallas kernels, body(): pl.pallas_call(kernel, out_shape=(jax.ShapeDtypeStruct((3, N // ROWS, N /...  77.3 us
    unnamed x4, local copies, waits for them, and re-layouts  3.24 us

profile of v1, /device:TPU:1, one launch (start us, length us, event | category | flops | bytes accessed | tf_op | source)
XLA Modules:
  0.0 81.1 jit_solution(12582001368335212055)
XLA Ops:
  0.6 77.3 %shard_map.86 = (bf16[3,32,16,512]{3,2,1,0:T(8,128)(2,1)}, f32[1,2,8]{2,1,0:T(2,128)}) custom-call(bf16[11,11,3,704]{3,2,1,0:T(4,128)(2,1)} %bitcast.1, f32[8]{0:T(128)} %waves_hbm.1, f32[32]{0:T(128)} %polar_hbm.1, f32[32]{0:T(128)} %azimuth_hbm.1, bf16[2,512,384]{2,1,0:T(8,128)(2,1)} %constant.6.clone.one_hbm, bf16[1024,512]{1,0:T(8,128)(2,1)} %constant.7.clone.two_hbm, ...), custom_call_target="tpu_custom_call" | custom-call | tf_op jit(solution)/shard_map/pallas_call | solution.py:361
  77.9 0.0 copy-start
  77.9 2.7 %copy.11 = bf16[3,32,16,512]{3,2,1,0:T(8,128)(2,1)} copy(bf16[3,32,16,512]{3,2,1,0:T(8,128)(2,1)} %get-tuple-element.4) | data formatting | bytes 3145728
  80.6 0.0 copy-done
  80.6 0.6 copy.12
Async XLA Ops:
  77.9 2.7 %copy-start = (f32[1,2,8]{2,1,0:T(2,128)S(1)}, f32[1,2,8]{2,1,0:T(2,128)}, u32[]{:S(2)}) copy-start(f32[1,2,8]{2,1,0:T(2,128)} %get-tuple-element.5) | copy-start | bytes 196

commit v2 on v1

--- a/solution.py
+++ b/solution.py
@@ -86,12 +86,12 @@
 
 def kernel(
     modes_hbm, waves_hbm, polar_hbm, azimuth_hbm, one_hbm, two_hbm, three_hbm,
-    vel_hbm, far_ref,
+    vel_ref, far_ref,
     waves_ref, polar_ref, azimuth_ref,
     modes, padded, one, two, three, picked_re, picked_im, sent, got, lhs, mid,
-    rsent, rgot, lhs_x, field, vel, phase, cos_yz, sin_yz, weights, mixed, spectrum,
+    rsent, rgot, lhs_x, field, phase, cos_yz, sin_yz, weights, mixed, spectrum,
     fsent, fgot, gsent, ggot,
-    load_sem, csend, crecv, rsend, rrecv, out_sem, fsend_sem, frecv_sem, gsend_sem, grecv_sem,
+    load_sem, csend, crecv, rsend, rrecv, fsend_sem, frecv_sem, gsend_sem, grecv_sem,
 ):
     row = lax.axis_index("row")
     col = lax.axis_index("col")
@@ -277,8 +277,11 @@
                     block = rgot[e, :, p * 2 + y_upper].reshape(256, 128)
                     lhs_x[y_upper * 128 : (y_upper + 1) * 128, p * 256 : (p + 1) * 256] = nt(turn, block).astype(BF)
             field[c] = jnp.dot(lhs_x[...], three[...], preferred_element_type=F32)
-            vel[e] = field[c].reshape(32, 8, N).astype(BF)
-            pltpu.make_async_copy(vel.at[e], vel_hbm.at[c, :, pl.ds(h * 8, 8), :], out_sem.at[e]).start()
+            for k in range(2):
+
+                @pl.when(h == k)
+                def _():
+                    vel_ref[c, :, k * 8 : k * 8 + 8, :] = field[c].reshape(32, 8, N).astype(BF)
 
             def component(g, carry):
                 stress = (field[c] * field[g]).astype(BF)
@@ -345,7 +348,6 @@
         pltpu.make_async_copy(
             rsent.at[c, pl.ds(0, ROWS - 1)], rsent.at[c, pl.ds(0, ROWS - 1)], rsend.at[c]
         ).wait()
-        pltpu.make_async_copy(vel.at[c], vel_hbm.at[c % 3, :, pl.ds(c // 3 * 8, 8), :], out_sem.at[c]).wait()
     pltpu.make_async_copy(
         fsent.at[pl.ds(0, COLS - 1)], fsent.at[pl.ds(0, COLS - 1)], fsend_sem
     ).wait()
@@ -361,11 +363,11 @@
     return pl.pallas_call(
         kernel,
         out_shape=(
-            jax.ShapeDtypeStruct((3, N // ROWS, N // COLS, N), BF),
-            jax.ShapeDtypeStruct((1, 2, FREQS), F32),
+            pltpu.VMEM((3, N // ROWS, N // COLS, N), BF),
+            pltpu.VMEM((1, 2, FREQS), F32),
         ),
         in_specs=[hbm] * 7,
-        out_specs=(pl.BlockSpec(memory_space=pl.ANY), pl.BlockSpec(memory_space=pltpu.VMEM)),
+        out_specs=(pl.BlockSpec(memory_space=pltpu.VMEM), pl.BlockSpec(memory_space=pltpu.VMEM)),
         scratch_shapes=[
             pltpu.SMEM((FREQS,), F32),
             pltpu.SMEM((DIRS,), F32),
@@ -385,7 +387,6 @@
             pltpu.VMEM((6, ROWS, 4, 16, 128), BF),
             pltpu.VMEM((256, N), BF),
             pltpu.VMEM((3, 256, N), F32),
-            pltpu.VMEM((6, 32, 8, N), BF),
             pltpu.VMEM((N, N), BF),
             pltpu.VMEM((N, 256), F32),
             pltpu.VMEM((N, 256), F32),
@@ -401,14 +402,13 @@
             dma((6,)),
             dma((6,)),
             dma((6,)),
-            dma((6,)),
             dma,
             dma,
             dma,
             dma,
         ],
         compiler_params=pltpu.CompilerParams(
-            collective_id=0, has_side_effects=True, vmem_limit_bytes=67043328
+            collective_id=0, has_side_effects=True, vmem_limit_bytes=65000000
         ),
     )(jnp.transpose(velocity_modes, (1, 2, 0, 3)), wavenumbers, polar, azimuth, jnp.asarray(one), jnp.asarray(two), jnp.asarray(three))
 

time: 81.3 us -> 79.1 us (0.973)
  local copies, waits for them, and re-layouts: 3.24 us -> 1.71 us
    unnamed x4 -> x2, local copies, waits for them, and re-layouts: 3.24 us -> 1.71 us
where the time goes in v2:
time: 79.1 us; the launch traced here: 79 us
  Pallas kernels  76.7 us (97%)
  local copies, waits for them, and re-layouts  1.71 us (2%)
    pallas_call x1, Pallas kernels, body(): pl.pallas_call(kernel, out_shape=(pltpu.VMEM((3, N // ROWS, N // COLS, N)...  76.7 us
    unnamed x2, local copies, waits for them, and re-layouts  1.71 us

profile of v2, /device:TPU:1, one launch (start us, length us, event | category | flops | bytes accessed | tf_op | source)
XLA Modules:
  0.0 79.0 jit_solution(3445271113023132247)
XLA Ops:
  0.6 76.7 %shard_map.86 = (bf16[3,32,16,512]{3,2,1,0:T(8,128)(2,1)S(1)}, f32[1,2,8]{2,1,0:T(2,128)S(1)}) custom-call(bf16[11,11,3,704]{3,2,1,0:T(4,128)(2,1)} %bitcast.1, f32[8]{0:T(128)} %waves_hbm.1, f32[32]{0:T(128)} %polar_hbm.1, f32[32]{0:T(128)} %azimuth_hbm.1, bf16[2,512,384]{2,1,0:T(8,128)(2,1)} %constant.6.clone.one_hbm, ...), custom_call_target="tpu_custom_call" | custom-call | tf_op jit(solution)/shard_map/pallas_call | solution.py:363
  77.3 1.1 %copy.11 = bf16[3,32,16,512]{3,2,1,0:T(8,128)(2,1)} copy(bf16[3,32,16,512]{3,2,1,0:T(8,128)(2,1)S(1)} %get-tuple-element.2) | data formatting | bytes 3145728
  78.4 0.6 copy.12

commit v3 on v2

--- a/solution.py
+++ b/solution.py
@@ -28,14 +28,14 @@
     sin = np.sin(2.0 * np.pi / N * np.arange(N))
     waves = np.arange(M) - M // 2
     grid = (waves[None, :] * np.arange(N)[:, None]) % N
-    base = np.stack([cos[grid], sin[grid]], 0).reshape(2, COLS, 2, 8, M)
-    one = np.zeros((2, 2, COLS, 8, 384), np.float32)
-    one[..., :M] = base.transpose(0, 2, 1, 3, 4)
-    one = one.reshape(2, N, 384)
+    base = np.stack([cos[grid], sin[grid]], 0).reshape(2, COLS, 4, 4, M)
+    one = np.zeros((4, COLS, 2, 4, 384), np.float32)
+    one[..., :M] = base.transpose(2, 1, 0, 3, 4)
+    one = one.reshape(2 * N, 384)
     grid = (waves[:, None] * np.arange(N)[None, :]) % N
-    base = np.zeros((2, COLS, 16, N))
+    base = np.zeros((2, COLS, 12, N))
     base[:, :, :KL] = np.stack([cos[grid], -sin[grid]], 0).reshape(2, COLS, KL, N)
-    two = base.reshape(2, COLS, 2, 8, 2, 8, 2, 16).transpose(2, 1, 0, 3, 4, 6, 7, 5).reshape(2 * N, N)
+    two = base.reshape(2, COLS, 3, 4, 4, 4, 32).transpose(2, 1, 0, 3, 4, 6, 5).reshape(24 * COLS, N)
     half = np.arange(KX)
     grid = (half[:, None] * np.arange(N)[None, :]) % N
     factor = np.where(half == 0, 1.0, 2.0)[:, None]
@@ -57,10 +57,10 @@
 def swapped(tiles):
     lane = iota((16, 128), 1)
     tiles = list(tiles)
-    for bit in range(3):
+    for bit in range(2):
         step = 1 << bit
         low = lax.rem(lane // step, 2) == 0
-        for i in range(8):
+        for i in range(4):
             if (i // step) % 2:
                 continue
             a, b = tiles[i], tiles[i + step]
@@ -132,45 +132,57 @@
     loads[1].wait()
     nt = functools.partial(lax.dot_general, dimension_numbers=NT, preferred_element_type=F32)
 
-    def along_z(h, carry):
-        cosine = one[0, pl.ds(h * 256, 256), :]
-        sine = one[1, pl.ds(h * 256, 256), :]
-        x_re = nt(cosine, picked_re[...]) - nt(sine, picked_im[...])
-        x_im = nt(sine, picked_re[...]) + nt(cosine, picked_im[...])
-        x = jnp.concatenate([x_re.reshape(COLS, 8, 384), x_im.reshape(COLS, 8, 384)], 1).astype(BF)
+    def quarter_turn(x):
+        moved = pltpu.roll(x, 4, 1)
+        return jnp.where(iota(x.shape, 1) < 4, -moved, moved)
+
+    def along_z(q, carry):
+        part = one[pl.ds(pl.multiple_of(q * 256, 256), 256), :]
+        x = nt(part, picked_re[...]).reshape(COLS, 8, 384)
+        x = (x + quarter_turn(nt(part, picked_im[...]).reshape(COLS, 8, 384))).astype(BF)
         for c in range(3):
-            sent[h * 3 + c] = x[:, :, c * 128 : (c + 1) * 128]
-
-        @pl.when(h == 0)
+            sent[q, :, c] = x[:, :, c * 128 : (c + 1) * 128]
+
+        @pl.when(q == 0)
         def _():
             pl.semaphore_wait(barrier, COLS + ROWS - 2)
 
-        def send_col(c, carry):
-            n = h * 3 + c
+        @pl.when(q < 3)
+        def _():
             for peer in peers:
                 pltpu.make_async_remote_copy(
-                    src_ref=sent.at[n, peer], dst_ref=got.at[n, col],
-                    send_sem=csend.at[n], recv_sem=crecv.at[n],
+                    src_ref=sent.at[q, peer], dst_ref=got.at[q, col],
+                    send_sem=csend.at[q], recv_sem=crecv.at[q],
                     device_id=(row, peer), device_id_type=MESH,
                 ).start()
-            got[n, pl.ds(col, 1)] = sent[n, pl.ds(col, 1)]
-            return carry
-
-        lax.fori_loop(0, 3, send_col, 0)
+
+        @pl.when(q == 3)
+        def _():
+            def send_col(c, carry):
+                for peer in peers:
+                    pltpu.make_async_remote_copy(
+                        src_ref=sent.at[3, peer, c], dst_ref=got.at[3, col, c],
+                        send_sem=csend.at[3 + c], recv_sem=crecv.at[3 + c],
+                        device_id=(row, peer), device_id_type=MESH,
+                    ).start()
+                return carry
+
+            lax.fori_loop(0, 3, send_col, 0)
+
+        got[q, pl.ds(col, 1)] = sent[q, pl.ds(col, 1)]
         return carry
 
-    lax.fori_loop(0, 2, along_z, 0)
+    lax.fori_loop(0, 4, along_z, 0)
 
     loads[2].wait()
 
     def fill_two(b, carry):
         base = pl.multiple_of(b * 64, 64)
-        half = two[pl.ds(base, 64), 0:N].astype(F32).reshape(4, 2, 8, N)
-        other = jnp.concatenate([-half[:, 1:2], half[:, 0:1]], 1)
-        two[pl.ds(base, 64), N : 2 * N] = other.reshape(64, N).astype(BF)
+        half = two[pl.ds(base, 64), 0:N].astype(F32).reshape(8, 8, N)
+        two[pl.ds(base, 64), N : 2 * N] = quarter_turn(half).reshape(64, N).astype(BF)
         return carry
 
-    lax.fori_loop(0, 16, fill_two, 0)
+    lax.fori_loop(0, 12, fill_two, 0)
     for load in loads[4:]:
         load.wait()
 
@@ -203,9 +215,9 @@
         angle = wave_1 * (one_1 * (index.astype(F32) * unit))
         phase[pl.ds(base, 32), 0:256] = jnp.cos(angle).astype(BF)
         phase[pl.ds(base, 32), 256:512] = (-jnp.sin(angle)).astype(BF)
-        part = lax.rem(index, 256)
-        y_pos = (row * 32 + part // 8).astype(F32) * unit
-        z_pos = (col * 16 + (index // 256) * 8 + lax.rem(part, 8)).astype(F32) * unit
+        part = lax.rem(index, 128)
+        y_pos = (row * 32 + part // 4).astype(F32) * unit
+        z_pos = (col * 16 + (index // 128) * 4 + lax.rem(part, 4)).astype(F32) * unit
         angle = wave_1 * (two_1 * y_pos) + wave_1 * (three_1 * z_pos)
         cos_yz[pl.ds(base, 32), :] = jnp.cos(angle)
         sin_yz[pl.ds(base, 32), :] = jnp.sin(angle)
@@ -221,38 +233,40 @@
     loads[3].wait()
 
     def step(n, carry):
-        @pl.when(n < 6)
+        @pl.when(n < 12)
         def _():
-            pltpu.make_async_copy(
-                got.at[n, pl.ds(0, COLS - 1)], got.at[n, pl.ds(0, COLS - 1)], crecv.at[n]
-            ).wait()
-
-            def regroup(pair, carry):
-                for k in range(2):
-                    t = pair * 2 + k
-                    lines = got[n, pl.ds(t * 8, 8)].reshape(128, 128)
-                    turned = nt(spread, lines).astype(BF)
-                    zero = jnp.zeros((16, 128), BF)
-                    tiles = [turned[m * 16 : m * 16 + 16] for m in range(KL)] + [zero] * (16 - KL)
-                    for m, tile in enumerate(swapped(tiles[:8])):
-                        lhs[t, m * 16 : m * 16 + 16, :] = tile
-                    for m, tile in enumerate(swapped(tiles[8:])):
-                        lhs[t + 4, m * 16 : m * 16 + 16, :] = tile
-                return carry
-
-            lax.fori_loop(0, 2, regroup, 0)
-            wide = jnp.concatenate([lhs[t] for t in range(8)], 1)
+            q = lax.div(n, 3)
+            c = n - 3 * q
+
+            @pl.when((q < 3) & (c == 0))
+            def _():
+                pltpu.make_async_copy(
+                    got.at[q, pl.ds(0, COLS - 1)], got.at[q, pl.ds(0, COLS - 1)], crecv.at[q]
+                ).wait()
+
+            @pl.when(q == 3)
+            def _():
+                pltpu.make_async_copy(
+                    got.at[3, pl.ds(0, COLS - 1), c], got.at[3, pl.ds(0, COLS - 1), c], crecv.at[3 + c]
+                ).wait()
+
+            for t in range(2):
+                lines = got[q, t * 16 : t * 16 + 16, c].astype(F32).reshape(128, 128).astype(BF)
+                turned = nt(spread, lines).astype(BF)
+                tiles = [turned[m * 16 : m * 16 + 16] for m in range(KL)] + [jnp.zeros((16, 128), BF)]
+                for k in range(3):
+                    for m, tile in enumerate(swapped(tiles[4 * k : 4 * k + 4])):
+                        lhs[2 * k + t, m * 16 : m * 16 + 16, :] = tile
+            wide = jnp.concatenate([lhs[t] for t in range(6)], 1)
             out = jnp.dot(wide, two[...], preferred_element_type=F32)
             for t in range(8):
                 mid[t] = out[:, t * 128 : (t + 1) * 128].astype(BF)
 
-            def regroup_row(part, carry):
-                for upper in range(2):
-                    for y_upper in range(2):
-                        t = part * 4 + upper * 2 + y_upper
-                        tiles = [mid[t, k * 16 : k * 16 + 16, :] for k in range(8)]
-                        for k, tile in enumerate(swapped(tiles)):
-                            rsent[n, upper * 8 + k, part * 2 + y_upper] = tile
+            def regroup_row(p, carry):
+                for upper in range(4):
+                    tiles = [mid[p * 4 + upper, k * 16 : k * 16 + 16, :] for k in range(4)]
+                    for k, tile in enumerate(swapped(tiles)):
+                        rsent[n, upper * 4 + k, p] = tile
                 return carry
 
             lax.fori_loop(0, 2, regroup_row, 0)
@@ -264,27 +278,33 @@
                 ).start()
             rgot[n, pl.ds(row, 1)] = rsent[n, pl.ds(row, 1)]
 
-        @pl.when(n > 0)
+        @pl.when(n > 2)
         def _():
-            e = n - 1
-            h = lax.div(e, 3)
-            c = e - 3 * h
+            e = n - 3
+            q = lax.div(e, 3)
+            c = e - 3 * q
+            odd = lax.rem(q, 2)
             pltpu.make_async_copy(
                 rgot.at[e, pl.ds(0, ROWS - 1)], rgot.at[e, pl.ds(0, ROWS - 1)], rrecv.at[e]
             ).wait()
-            for y_upper in range(2):
-                for p in range(2):
-                    block = rgot[e, :, p * 2 + y_upper].reshape(256, 128)
-                    lhs_x[y_upper * 128 : (y_upper + 1) * 128, p * 256 : (p + 1) * 256] = nt(turn, block).astype(BF)
-            field[c] = jnp.dot(lhs_x[...], three[...], preferred_element_type=F32)
+            for p in range(2):
+                block = rgot[e, :, p].reshape(256, 128)
+                lhs_x[:, p * 256 : (p + 1) * 256] = nt(turn, block).astype(BF)
+            field[odd, c] = jnp.dot(lhs_x[...], three[...], preferred_element_type=F32)
             for k in range(2):
 
-                @pl.when(h == k)
+                @pl.when(q == 2 * k + 1)
                 def _():
-                    vel_ref[c, :, k * 8 : k * 8 + 8, :] = field[c].reshape(32, 8, N).astype(BF)
+                    a = field[0, c].reshape(16, 8, N)
+                    b = field[1, c].reshape(16, 8, N)
+                    low = iota((16, 8, N), 1) < 4
+                    even_y = jnp.where(low, a, pltpu.roll(b, 4, 1))
+                    odd_y = jnp.where(low, pltpu.roll(a, 4, 1), b)
+                    both = jnp.concatenate([even_y.reshape(16, 1, 8, N), odd_y.reshape(16, 1, 8, N)], 1)
+                    vel_ref[c, :, k * 8 : k * 8 + 8, :] = both.reshape(32, 8, N).astype(BF)
 
             def component(g, carry):
-                stress = (field[c] * field[g]).astype(BF)
+                stress = (field[odd, c] * field[odd, g]).astype(BF)
                 lines = jnp.dot(stress, phase[...], preferred_element_type=F32)
                 mixed[...] += weights[c, g, 0:1, :] * lines
                 return carry
@@ -294,14 +314,15 @@
             @pl.when(c == 2)
             def _():
                 re, im = mixed[:, 0:256], mixed[:, 256:512]
-                cosine, sine = cos_yz[pl.ds(h * 256, 256), :], sin_yz[pl.ds(h * 256, 256), :]
+                base = pl.multiple_of(q * 128, 128)
+                cosine, sine = cos_yz[pl.ds(base, 128), :], sin_yz[pl.ds(base, 128), :]
                 spectrum[0:1, :] += jnp.sum(re * cosine + im * sine, axis=0, keepdims=True)
                 spectrum[1:2, :] += jnp.sum(im * cosine - re * sine, axis=0, keepdims=True)
                 mixed[...] = jnp.zeros_like(mixed)
 
         return carry
 
-    lax.fori_loop(0, 7, step, 0)
+    lax.fori_loop(0, 15, step, 0)
 
     sum_re, sum_im = spectrum[0:1, :], spectrum[1:2, :]
     mine = lax.rem(iota((DIRS, 256), 1), DIRS) == iota((DIRS, 256), 0)
@@ -341,12 +362,17 @@
     far_ref[0, 0:1, :] = total[:, 0:FREQS]
     far_ref[0, 1:2, :] = total[:, FREQS : 2 * FREQS]
 
-    for c in range(6):
+    for q in range(3):
         pltpu.make_async_copy(
-            sent.at[c, pl.ds(0, COLS - 1)], sent.at[c, pl.ds(0, COLS - 1)], csend.at[c]
+            sent.at[q, pl.ds(0, COLS - 1)], sent.at[q, pl.ds(0, COLS - 1)], csend.at[q]
         ).wait()
+    for c in range(3):
         pltpu.make_async_copy(
-            rsent.at[c, pl.ds(0, ROWS - 1)], rsent.at[c, pl.ds(0, ROWS - 1)], rsend.at[c]
+            sent.at[3, pl.ds(0, COLS - 1), c], sent.at[3, pl.ds(0, COLS - 1), c], csend.at[3 + c]
+        ).wait()
+    for n in range(12):
+        pltpu.make_async_copy(
+            rsent.at[n, pl.ds(0, ROWS - 1)], rsent.at[n, pl.ds(0, ROWS - 1)], rsend.at[n]
         ).wait()
     pltpu.make_async_copy(
         fsent.at[pl.ds(0, COLS - 1)], fsent.at[pl.ds(0, COLS - 1)], fsend_sem
@@ -374,24 +400,24 @@
             pltpu.SMEM((DIRS,), F32),
             pltpu.VMEM((KL, KL, 3, 2 * M), BF),
             pltpu.VMEM((488, 768), F32),
-            pltpu.VMEM((2, N, 384), BF),
-            pltpu.VMEM((2 * N, 2 * N), BF),
+            pltpu.VMEM((2 * N, 384), BF),
+            pltpu.VMEM((24 * COLS, 2 * N), BF),
             pltpu.VMEM((N, N), BF),
             pltpu.VMEM((384, 384), BF),
             pltpu.VMEM((384, 384), BF),
-            pltpu.VMEM((6, COLS, 16, 128), BF),
-            pltpu.VMEM((6, COLS, 16, 128), BF),
-            pltpu.VMEM((8, 128, 128), BF),
-            pltpu.VMEM((8, 128, 128), BF),
-            pltpu.VMEM((6, ROWS, 4, 16, 128), BF),
-            pltpu.VMEM((6, ROWS, 4, 16, 128), BF),
-            pltpu.VMEM((256, N), BF),
-            pltpu.VMEM((3, 256, N), F32),
+            pltpu.VMEM((4, COLS, 3, 8, 128), BF),
+            pltpu.VMEM((4, COLS, 3, 8, 128), BF),
+            pltpu.VMEM((6, 64, 128), BF),
+            pltpu.VMEM((8, 64, 128), BF),
+            pltpu.VMEM((12, ROWS, 2, 16, 128), BF),
+            pltpu.VMEM((12, ROWS, 2, 16, 128), BF),
+            pltpu.VMEM((128, N), BF),
+            pltpu.VMEM((2, 3, 128, N), F32),
             pltpu.VMEM((N, N), BF),
             pltpu.VMEM((N, 256), F32),
             pltpu.VMEM((N, 256), F32),
             pltpu.VMEM((3, 3, 8, N), F32),
-            pltpu.VMEM((256, N), F32),
+            pltpu.VMEM((128, N), F32),
             pltpu.VMEM((8, 256), F32),
             pltpu.VMEM((COLS, 1, 128), F32),
             pltpu.VMEM((COLS, 1, 128), F32),
@@ -400,8 +426,8 @@
             dma((7,)),
             dma((6,)),
             dma((6,)),
-            dma((6,)),
-            dma((6,)),
+            dma((12,)),
+            dma((12,)),
             dma,
             dma,
             dma,

time: 79.1 us -> 79.4 us (level)
  no operation moved by 1% of the time
where the time goes in v3:
time: 79.4 us; the launch traced here: 79.2 us
  Pallas kernels  76.9 us (97%)
  local copies, waits for them, and re-layouts  1.71 us (2%)
    pallas_call x1, Pallas kernels, body(): pl.pallas_call(kernel, out_shape=(pltpu.VMEM((3, N // ROWS, N // COLS, N)...  76.9 us
    unnamed x2, local copies, waits for them, and re-layouts  1.71 us

profile of v3, /device:TPU:1, one launch (start us, length us, event | category | flops | bytes accessed | tf_op | source)
XLA Modules:
  0.0 79.2 jit_solution(12608605140643063334)
XLA Ops:
  0.6 76.9 %shard_map.86 = (bf16[3,32,16,512]{3,2,1,0:T(8,128)(2,1)S(1)}, f32[1,2,8]{2,1,0:T(2,128)S(1)}) custom-call(bf16[11,11,3,704]{3,2,1,0:T(4,128)(2,1)} %bitcast.1, f32[8]{0:T(128)} %waves_hbm.1, f32[32]{0:T(128)} %polar_hbm.1, f32[32]{0:T(128)} %azimuth_hbm.1, bf16[1024,384]{1,0:T(8,128)(2,1)} %constant.6.clone.one_hbm, ...), custom_call_target="tpu_custom_call" | custom-call | tf_op jit(solution)/shard_map/pallas_call | solution.py:389
  77.5 1.1 %copy.11 = bf16[3,32,16,512]{3,2,1,0:T(8,128)(2,1)} copy(bf16[3,32,16,512]{3,2,1,0:T(8,128)(2,1)S(1)} %get-tuple-element.2) | data formatting | bytes 3145728
  78.7 0.6 copy.12

commit v4 on v2

--- a/solution.py
+++ b/solution.py
@@ -84,6 +84,20 @@
     return peers
 
 
+def row_peers_of(row):
+    x = lax.div(row, 8)
+    y = lax.div(row - 8 * x, 2)
+    core = row - 8 * x - 2 * y
+    peers = []
+    for dx in (1, 0):
+        for dy in (2, 1, 3, 0):
+            there = (1 - x if dx else x) * 8 + lax.rem(y + dy, 4) * 2
+            for dc in (1, 0):
+                if dx or dy or dc:
+                    peers.append(there + (1 - core if dc else core))
+    return peers
+
+
 def kernel(
     modes_hbm, waves_hbm, polar_hbm, azimuth_hbm, one_hbm, two_hbm, three_hbm,
     vel_ref, far_ref,
@@ -96,7 +110,7 @@
     row = lax.axis_index("row")
     col = lax.axis_index("col")
     peers = col_peers(col)
-    row_peers = [lax.rem(row + k, ROWS) for k in range(1, ROWS)]
+    row_peers = row_peers_of(row)
 
     barrier = pltpu.get_barrier_semaphore()
     for peer in peers:

time: 79.1 us -> 79.4 us (level)
  no operation moved by 1% of the time
where the time goes in v4:
time: 79.4 us; the launch traced here: 79.3 us
  Pallas kernels  76.9 us (97%)
  local copies, waits for them, and re-layouts  1.71 us (2%)
    pallas_call x1, Pallas kernels, body(): pl.pallas_call(kernel, out_shape=(pltpu.VMEM((3, N // ROWS, N // COLS, N)...  76.9 us
    unnamed x2, local copies, waits for them, and re-layouts  1.71 us

profile of v4, /device:TPU:1, one launch (start us, length us, event | category | flops | bytes accessed | tf_op | source)
XLA Modules:
  0.0 79.3 jit_solution(3194917875845906958)
XLA Ops:
  0.6 76.9 %shard_map.86 = (bf16[3,32,16,512]{3,2,1,0:T(8,128)(2,1)S(1)}, f32[1,2,8]{2,1,0:T(2,128)S(1)}) custom-call(bf16[11,11,3,704]{3,2,1,0:T(4,128)(2,1)} %bitcast.1, f32[8]{0:T(128)} %waves_hbm.1, f32[32]{0:T(128)} %polar_hbm.1, f32[32]{0:T(128)} %azimuth_hbm.1, bf16[2,512,384]{2,1,0:T(8,128)(2,1)} %constant.6.clone.one_hbm, ...), custom_call_target="tpu_custom_call" | custom-call | tf_op jit(solution)/shard_map/pallas_call | solution.py:377
  77.6 1.1 %copy.11 = bf16[3,32,16,512]{3,2,1,0:T(8,128)(2,1)} copy(bf16[3,32,16,512]{3,2,1,0:T(8,128)(2,1)S(1)} %get-tuple-element.2) | data formatting | bytes 3145728
  78.7 0.6 copy.12

commit v5 on v2

--- a/solution.py
+++ b/solution.py
@@ -264,9 +264,9 @@
                 ).start()
             rgot[n, pl.ds(row, 1)] = rsent[n, pl.ds(row, 1)]
 
-        @pl.when(n > 0)
+        @pl.when(n > 1)
         def _():
-            e = n - 1
+            e = n - 2
             h = lax.div(e, 3)
             c = e - 3 * h
             pltpu.make_async_copy(
@@ -301,7 +301,7 @@
 
         return carry
 
-    lax.fori_loop(0, 7, step, 0)
+    lax.fori_loop(0, 8, step, 0)
 
     sum_re, sum_im = spectrum[0:1, :], spectrum[1:2, :]
     mine = lax.rem(iota((DIRS, 256), 1), DIRS) == iota((DIRS, 256), 0)

time: 79.1 us -> 79.1 us (level)
  no operation moved by 1% of the time
where the time goes in v5:
time: 79.1 us; the launch traced here: 79 us
  Pallas kernels  76.7 us (97%)
  local copies, waits for them, and re-layouts  1.71 us (2%)
    pallas_call x1, Pallas kernels, body(): pl.pallas_call(kernel, out_shape=(pltpu.VMEM((3, N // ROWS, N // COLS, N)...  76.7 us
    unnamed x2, local copies, waits for them, and re-layouts  1.71 us

profile of v5, /device:TPU:1, one launch (start us, length us, event | category | flops | bytes accessed | tf_op | source)
XLA Modules:
  0.0 79.0 jit_solution(5390892551578607556)
XLA Ops:
  0.6 76.7 %shard_map.86 = (bf16[3,32,16,512]{3,2,1,0:T(8,128)(2,1)S(1)}, f32[1,2,8]{2,1,0:T(2,128)S(1)}) custom-call(bf16[11,11,3,704]{3,2,1,0:T(4,128)(2,1)} %bitcast.1, f32[8]{0:T(128)} %waves_hbm.1, f32[32]{0:T(128)} %polar_hbm.1, f32[32]{0:T(128)} %azimuth_hbm.1, bf16[2,512,384]{2,1,0:T(8,128)(2,1)} %constant.6.clone.one_hbm, ...), custom_call_target="tpu_custom_call" | custom-call | tf_op jit(solution)/shard_map/pallas_call | solution.py:363
  77.3 1.1 %copy.11 = bf16[3,32,16,512]{3,2,1,0:T(8,128)(2,1)} copy(bf16[3,32,16,512]{3,2,1,0:T(8,128)(2,1)S(1)} %get-tuple-element.2) | data formatting | bytes 3145728
  78.4 0.6 copy.12
